TPU v7x, 32 devices: a whole 2x2x4 slice. The times are simulated.
32 devices in a mesh: wide: 8 (over z, x), narrow: 4 (over y, core).
Axes of the slice: x: 2, y: 2, z: 4, core: 2. Of those that a mesh axis runs over, the one named last changes fastest.
Arguments:
- payload: bfloat16 [131072, 128], P(('wide', 'narrow')), may hold values from -6 to 6
- first_key: int32 [131072], P(('wide', 'narrow')), may hold values from 0 to 1073741823
- second_key: int32 [131072], P(('wide', 'narrow')), may hold values from 0 to 1073741823
- live: int32 [131072], P(('wide', 'narrow')), may hold values from 0 to 1
- first_bucket: int32 [131072], P(('wide', 'narrow')), may hold values from 0 to 7, as said below
- second_bucket: int32 [131072], P(('wide', 'narrow')), may hold values from 0 to 3
Outputs:
- group_mean: bfloat16 [131072, 128], P(('wide', 'narrow'))
- duplicate_count: int32 [], replicated
Inputs may be any that keep to these rules, and one draw needn't show every extreme that they name: Each device's rows name each pair (first_bucket, second_bucket) exactly 128 times; in every draw there is one bucket pair all of whose rows survive; other rows survive or not as `live` says.
All inputs are finite; a program needn't handle non-finite values.
Results may differ from a plain program's by a relative error of at most 0.001.
Values may be sent and summed in bfloat16 or wider, within the bound.
A program may use at most 64 MiB of HBM per device.

v0:
```python
import jax
import jax.numpy as jnp
from jax import lax
from jax.sharding import PartitionSpec as P


def pair_mask(row_one, row_two, row_live, col_one, col_two, col_live):
    return (
        (row_one[:, None] == col_one[None, :])
        & (row_two[:, None] == col_two[None, :])
        & (row_live[:, None] > 0)
        & (col_live[None, :] > 0)
    )


def on_device(payload, first_key, second_key, live, first_bucket, second_bucket):
    wide_count = lax.axis_size("wide")
    narrow_count = lax.axis_size("narrow")
    row_count, feature_cols = payload.shape
    slot_rows = row_count // (wide_count * narrow_count)
    owner = first_bucket * narrow_count + second_bucket
    sort_order = jnp.argsort(owner, stable=True)
    inverse = jnp.argsort(sort_order, stable=True)
    sent_rows = payload[sort_order].reshape(wide_count, narrow_count, slot_rows, feature_cols)
    shaped = (wide_count, narrow_count, slot_rows)
    tags = jnp.stack(
        [
            first_key[sort_order].reshape(shaped),
            second_key[sort_order].reshape(shaped),
            live[sort_order].reshape(shaped),
        ],
        axis=2,
    )
    got_rows, got_tags = (
        lax.all_to_all(
            lax.all_to_all(sent_rows, "wide", split_axis=0, concat_axis=0, tiled=True),
            "narrow",
            split_axis=1,
            concat_axis=1,
            tiled=True,
        ),
        lax.all_to_all(
            lax.all_to_all(tags, "wide", split_axis=0, concat_axis=0, tiled=True),
            "narrow",
            split_axis=1,
            concat_axis=1,
            tiled=True,
        ),
    )
    owner_rows = wide_count * narrow_count * slot_rows
    flat_rows = got_rows.reshape(owner_rows, feature_cols)
    keys_one = got_tags[:, :, 0, :].reshape(owner_rows)
    keys_two = got_tags[:, :, 1, :].reshape(owner_rows)
    alive = got_tags[:, :, 2, :].reshape(owner_rows)
    tile_rows = min(512, owner_rows)
    column_pos = lax.iota(jnp.int32, owner_rows)

    def full_block(block_index, running):
        group_means, duplicate_total = running
        block_start = block_index * tile_rows
        row_one = lax.dynamic_slice_in_dim(keys_one, block_start, tile_rows)
        row_two = lax.dynamic_slice_in_dim(keys_two, block_start, tile_rows)
        row_live = lax.dynamic_slice_in_dim(alive, block_start, tile_rows)
        same = pair_mask(row_one, row_two, row_live, keys_one, keys_two, alive)
        sums = jnp.dot(same.astype(jnp.bfloat16), flat_rows, preferred_element_type=jnp.float32)
        counts = jnp.sum(same.astype(jnp.float32), axis=1)
        row_pos = block_start + lax.iota(jnp.int32, tile_rows)
        earlier = same & (column_pos[None, :] < row_pos[:, None])
        duplicate_total = duplicate_total + jnp.sum(jnp.any(earlier, axis=1).astype(jnp.float32))
        block_mean = (sums / jnp.maximum(counts, 1.0)[:, None]).astype(jnp.bfloat16)
        group_means = lax.dynamic_update_slice_in_dim(group_means, block_mean, block_start, 0)
        return (group_means, duplicate_total)

    start_state = (jnp.zeros((owner_rows, feature_cols), jnp.bfloat16), jnp.zeros((), jnp.float32))
    group_means, duplicate_total = lax.fori_loop(
        0, owner_rows // tile_rows, full_block, start_state
    )
    back_rows = group_means.reshape(wide_count, narrow_count, slot_rows, feature_cols)
    returned = lax.all_to_all(
        lax.all_to_all(back_rows, "wide", split_axis=0, concat_axis=0, tiled=True),
        "narrow",
        split_axis=1,
        concat_axis=1,
        tiled=True,
    )
    group_mean = returned.reshape(row_count, feature_cols)[inverse]
    overall = lax.psum(duplicate_total, ("wide", "narrow"))
    return (group_mean, overall.astype(jnp.int32))


def solution(mesh):
    placed = (
        P(("wide", "narrow"), None),
        P(("wide", "narrow")),
        P(("wide", "narrow")),
        P(("wide", "narrow")),
        P(("wide", "narrow")),
        P(("wide", "narrow")),
    )
    return jax.shard_map(
        on_device,
        mesh=mesh,
        in_specs=placed,
        out_specs=(P(("wide", "narrow"), None), P()),
        check_vma=False,
    )
```

profile of v0, /device:TPU:0, one launch (start us, length us, event | category | flops | bytes accessed | tf_op | source)
XLA Modules:
  0.0 326.9 jit_solution(6354122044880662689)
XLA Ops:
  0.7 0.8 multiply_add_fusion
  1.5 5.8 %sort.31 = (s32[4096]{0:T(1024)}, s32[4096]{0:T(1024)S(1)}) sort(s32[4096]{0:T(1024)S(1)} %multiply_add_fusion, s32[4096]{0:T(1024)S(1)} %iota.19), dimensions={0}, to_apply=%region_0.0 | sort | flops 49152 | bytes 65536 | tf_op jit(solution)/shard_map/jit(argsort)/sort | solution.py:22
  7.3 23.0 %gather_fusion.2 = s32[4096]{0:T(1024)S(1)} fusion(s32[4096]{0:T(1024)S(1)} %copy-done.1, s32[4096]{0:T(1024)S(1)} %fusion.6), kind=kCustom, calls=%fused_computation.2 | custom fusion | bytes 49152 | tf_op jit(solution)/shard_map/gather | solution.py:30
  30.4 23.0 %gather_fusion.1 = s32[4096]{0:T(1024)S(1)} fusion(s32[4096]{0:T(1024)S(1)} %copy-done.2, s32[4096]{0:T(1024)S(1)} %fusion.6), kind=kCustom, calls=%fused_computation.1 | custom fusion | bytes 49152 | tf_op jit(solution)/shard_map/gather | solution.py:29
  53.4 23.0 %gather_fusion = s32[4096]{0:T(1024)S(1)} fusion(s32[4096]{0:T(1024)S(1)} %copy-done.3, s32[4096]{0:T(1024)S(1)} %fusion.6), kind=kCustom, calls=%fused_computation | custom fusion | bytes 49152 | tf_op jit(solution)/shard_map/gather | solution.py:28
  77.1 7.3 %all-to-all-start = ((s32[8,4,3,128]{3,1,2,0:T(4,128)}), s32[8,4,3,128]{3,1,2,0:T(4,128)S(1)}, u32[]{:S(2)}, u32[]{:S(2)}) async-start(s32[8,4,3,128]{3,1,2,0:T(4,128)} %pad_add_fusion), calls=%async_computation | async-start | bytes 98304 | tf_op jit(solution)/shard_map/all_to_all | solution.py:43
  84.4 15.0 %gather_fusion.3 = bf16[4096,128]{1,0:T(8,128)(2,1)} fusion(bf16[4096,128]{1,0:T(8,128)(2,1)S(1)} %copy-done, s32[4096]{0:T(1024)S(1)} %fusion.6), kind=kCustom, calls=%fused_computation.3 | custom fusion | bytes 2113536 | tf_op jit(solution)/shard_map/gather | solution.py:24
  99.4 6.0 %all-to-all-start.2 = ((bf16[8,4,128,128]{3,2,1,0:T(8,128)(2,1)}), bf16[8,4,128,128]{3,2,1,0:T(8,128)(2,1)S(1)}, u32[]{:S(2)}, u32[]{:S(2)}) async-start(bf16[8,4,128,128]{3,2,1,0:T(8,128)(2,1)} %bitcast.6), calls=%async_computation.2 | async-start | bytes 2097152 | tf_op jit(solution)/shard_map/all_to_all | solution.py:36
  106.0 24.8 %all-to-all-done.2 = bf16[8,4,128,128]{3,2,1,0:T(8,128)(2,1)S(1)} async-done(((bf16[8,4,128,128]{3,2,1,0:T(8,128)(2,1)}), bf16[8,4,128,128]{3,2,1,0:T(8,128)(2,1)S(1)}, u32[]{:S(2)}, u32[]{:S(2)}) %all-to-all-start.2) | async-done | bytes 1048608 | tf_op jit(solution)/shard_map/all_to_all | solution.py:36
  130.8 3.3 %all-to-all-start.1 = ((s32[8,4,3,128]{3,0,2,1:T(8,128)}), s32[8,4,3,128]{3,0,2,1:T(8,128)S(1)}, u32[]{:S(2)}, u32[]{:S(2)}) async-start(s32[8,4,3,128]{3,0,2,1:T(8,128)} %copy.38), calls=%async_computation.1 | async-start | bytes 98304 | tf_op jit(solution)/shard_map/all_to_all | solution.py:42
  134.1 1.0 copy.42
  135.1 3.0 all-to-all-done.1
  138.1 3.5 %all-to-all-start.3 = ((bf16[8,4,128,128]{3,2,0,1:T(8,128)(2,1)}), bf16[8,4,128,128]{3,2,0,1:T(8,128)(2,1)S(1)}, u32[]{:S(2)}, u32[]{:S(2)}) async-start(bf16[8,4,128,128]{3,2,0,1:T(8,128)(2,1)} %copy.42), calls=%async_computation.3 | async-start | bytes 2097152 | tf_op jit(solution)/shard_map/all_to_all | solution.py:35
  141.7 14.3 %all-to-all-done.3 = bf16[8,4,128,128]{3,2,0,1:T(8,128)(2,1)S(1)} async-done(((bf16[8,4,128,128]{3,2,0,1:T(8,128)(2,1)}), bf16[8,4,128,128]{3,2,0,1:T(8,128)(2,1)S(1)}, u32[]{:S(2)}, u32[]{:S(2)}) %all-to-all-start.3) | async-done | bytes 1048608 | tf_op jit(solution)/shard_map/all_to_all | solution.py:35
  156.0 1.1 copy.43
  157.1 1.1 broadcast_in_dim.30
  158.2 71.2 %while.16 = (s32[]{:T(128)}, bf16[4096,128]{1,0:T(8,128)(2,1)}, f32[]{:T(128)}, s32[4096]{0:T(1024)S(1)}, s32[8,4,1,128]{3,2,1,0:T(1,128)S(1)}, /*index=5*/s32[4...) while((s32[]{:T(128)}, bf16[4096,128]{1,0:T(8,128)(2,1)}, ...), condition=%wide.region_5.6_spmd.clone, body=%wide.region_1.5_spmd.clone.sunk | while | flops 557979136 | bytes 11751667 | solution.py:75
  158.4 4.1 %fusion.17 = (pred[512]{0:T(512)(128)(4,1)S(1)}, pred[512,4096]{1,0:T(32,128)(4,1)S(1)}) fusion(s32[512]{0:T(512)S(1)} %iota_add_fusion.2, pred[4096]{0:T(1024)(128)(4,1)S(1)} %bitcast.33, pred[512]{0:T(512)(128)(4,1)S(1)} %dynamic-slice_compare_fusion.2, s32[4096]{0:T(1024)S(1)} %bitcast.31, s32[512]{0:T(512)S(1)} %dynamic_slice.29, ...), kind=kLoop, calls=%fused_computation.9.clone.1 | loop fusion | flops 16776704 | bytes 2141184 | tf_op jit(solution)/shard_map/while/body/eval_jaxpr/reduce_or | solution.py:69
  162.6 0.7 convert_reduce_fusion.5
  164.0 1.0 convert_reduce_fusion.4
  165.2 1.9 fusion.18
  167.3 4.1 %fusion.17 = (pred[512]{0:T(512)(128)(4,1)S(1)}, pred[512,4096]{1,0:T(32,128)(4,1)S(1)}) fusion(s32[512]{0:T(512)S(1)} %iota_add_fusion.2, pred[4096]{0:T(1024)(128)(4,1)S(1)} %bitcast.33, pred[512]{0:T(512)(128)(4,1)S(1)} %dynamic-slice_compare_fusion.2, s32[4096]{0:T(1024)S(1)} %bitcast.31, s32[512]{0:T(512)S(1)} %dynamic_slice.29, ...), kind=kLoop, calls=%fused_computation.9.clone.1 | loop fusion | flops 16776704 | bytes 2141184 | tf_op jit(solution)/shard_map/while/body/eval_jaxpr/reduce_or | solution.py:69
  172.9 1.0 convert_reduce_fusion.4
  174.1 1.9 fusion.18
  176.2 4.1 %fusion.17 = (pred[512]{0:T(512)(128)(4,1)S(1)}, pred[512,4096]{1,0:T(32,128)(4,1)S(1)}) fusion(s32[512]{0:T(512)S(1)} %iota_add_fusion.2, pred[4096]{0:T(1024)(128)(4,1)S(1)} %bitcast.33, pred[512]{0:T(512)(128)(4,1)S(1)} %dynamic-slice_compare_fusion.2, s32[4096]{0:T(1024)S(1)} %bitcast.31, s32[512]{0:T(512)S(1)} %dynamic_slice.29, ...), kind=kLoop, calls=%fused_computation.9.clone.1 | loop fusion | flops 16776704 | bytes 2141184 | tf_op jit(solution)/shard_map/while/body/eval_jaxpr/reduce_or | solution.py:69
  181.8 1.0 convert_reduce_fusion.4
  183.0 1.9 fusion.18
  185.1 4.1 %fusion.17 = (pred[512]{0:T(512)(128)(4,1)S(1)}, pred[512,4096]{1,0:T(32,128)(4,1)S(1)}) fusion(s32[512]{0:T(512)S(1)} %iota_add_fusion.2, pred[4096]{0:T(1024)(128)(4,1)S(1)} %bitcast.33, pred[512]{0:T(512)(128)(4,1)S(1)} %dynamic-slice_compare_fusion.2, s32[4096]{0:T(1024)S(1)} %bitcast.31, s32[512]{0:T(512)S(1)} %dynamic_slice.29, ...), kind=kLoop, calls=%fused_computation.9.clone.1 | loop fusion | flops 16776704 | bytes 2141184 | tf_op jit(solution)/shard_map/while/body/eval_jaxpr/reduce_or | solution.py:69
  190.7 1.0 convert_reduce_fusion.4
  191.9 1.9 fusion.18
  194.0 4.1 %fusion.17 = (pred[512]{0:T(512)(128)(4,1)S(1)}, pred[512,4096]{1,0:T(32,128)(4,1)S(1)}) fusion(s32[512]{0:T(512)S(1)} %iota_add_fusion.2, pred[4096]{0:T(1024)(128)(4,1)S(1)} %bitcast.33, pred[512]{0:T(512)(128)(4,1)S(1)} %dynamic-slice_compare_fusion.2, s32[4096]{0:T(1024)S(1)} %bitcast.31, s32[512]{0:T(512)S(1)} %dynamic_slice.29, ...), kind=kLoop, calls=%fused_computation.9.clone.1 | loop fusion | flops 16776704 | bytes 2141184 | tf_op jit(solution)/shard_map/while/body/eval_jaxpr/reduce_or | solution.py:69
  199.6 1.0 convert_reduce_fusion.4
  200.8 1.9 fusion.18
  202.9 4.1 %fusion.17 = (pred[512]{0:T(512)(128)(4,1)S(1)}, pred[512,4096]{1,0:T(32,128)(4,1)S(1)}) fusion(s32[512]{0:T(512)S(1)} %iota_add_fusion.2, pred[4096]{0:T(1024)(128)(4,1)S(1)} %bitcast.33, pred[512]{0:T(512)(128)(4,1)S(1)} %dynamic-slice_compare_fusion.2, s32[4096]{0:T(1024)S(1)} %bitcast.31, s32[512]{0:T(512)S(1)} %dynamic_slice.29, ...), kind=kLoop, calls=%fused_computation.9.clone.1 | loop fusion | flops 16776704 | bytes 2141184 | tf_op jit(solution)/shard_map/while/body/eval_jaxpr/reduce_or | solution.py:69
  208.5 1.0 convert_reduce_fusion.4
  209.7 1.9 fusion.18
  211.9 4.1 %fusion.17 = (pred[512]{0:T(512)(128)(4,1)S(1)}, pred[512,4096]{1,0:T(32,128)(4,1)S(1)}) fusion(s32[512]{0:T(512)S(1)} %iota_add_fusion.2, pred[4096]{0:T(1024)(128)(4,1)S(1)} %bitcast.33, pred[512]{0:T(512)(128)(4,1)S(1)} %dynamic-slice_compare_fusion.2, s32[4096]{0:T(1024)S(1)} %bitcast.31, s32[512]{0:T(512)S(1)} %dynamic_slice.29, ...), kind=kLoop, calls=%fused_computation.9.clone.1 | loop fusion | flops 16776704 | bytes 2141184 | tf_op jit(solution)/shard_map/while/body/eval_jaxpr/reduce_or | solution.py:69
  217.4 1.0 convert_reduce_fusion.4
  218.6 1.9 fusion.18
  220.8 4.1 %fusion.17 = (pred[512]{0:T(512)(128)(4,1)S(1)}, pred[512,4096]{1,0:T(32,128)(4,1)S(1)}) fusion(s32[512]{0:T(512)S(1)} %iota_add_fusion.2, pred[4096]{0:T(1024)(128)(4,1)S(1)} %bitcast.33, pred[512]{0:T(512)(128)(4,1)S(1)} %dynamic-slice_compare_fusion.2, s32[4096]{0:T(1024)S(1)} %bitcast.31, s32[512]{0:T(512)S(1)} %dynamic_slice.29, ...), kind=kLoop, calls=%fused_computation.9.clone.1 | loop fusion | flops 16776704 | bytes 2141184 | tf_op jit(solution)/shard_map/while/body/eval_jaxpr/reduce_or | solution.py:69
  226.3 1.0 convert_reduce_fusion.4
  227.5 1.9 fusion.18
  229.4 29.2 %all_to_all.30 = bf16[8,4,128,128]{3,2,1,0:T(8,128)(2,1)S(1)} all-to-all(bf16[8,4,128,128]{3,2,1,0:T(8,128)(2,1)} %bitcast.26), channel_id=1, replica_groups=mesh['wide'=8,'narrow'=4] {'wide'}, dimensions={0} | all-to-all | bytes 2097152 | tf_op jit(solution)/shard_map/all_to_all | solution.py:80
  258.6 1.0 copy.47
  259.6 3.5 %all-to-all-start.5 = ((bf16[8,4,128,128]{3,2,0,1:T(8,128)(2,1)}), bf16[8,4,128,128]{3,2,0,1:T(8,128)(2,1)S(1)}, u32[]{:S(2)}, u32[]{:S(2)}) async-start(bf16[8,4,128,128]{3,2,0,1:T(8,128)(2,1)} %copy.47), calls=%async_computation.5 | async-start | bytes 2097152 | tf_op jit(solution)/shard_map/all_to_all | solution.py:79
  263.2 5.8 %sort.32 = (s32[4096]{0:T(1024)}, s32[4096]{0:T(1024)S(1)}) sort(s32[4096]{0:T(1024)S(1)} %get-tuple-element.189, s32[4096]{0:T(1024)S(1)} %iota.21), dimensions={0}, to_apply=%region_6.7 | sort | flops 49152 | bytes 65536 | tf_op jit(solution)/shard_map/jit(argsort)/sort | solution.py:23
  269.0 40.9 %psum.7 = f32[]{:T(128)} all-reduce(f32[]{:T(128)} %get-tuple-element.192), channel_id=1, replica_groups=mesh['wide'=8,'narrow'=4] {'wide','narrow'}, use_global_device_ids=true, to_apply=%region_7.8 | all-reduce | flops 1 | bytes 8 | tf_op jit(solution)/shard_map/psum | solution.py:87
  310.7 15.0 %gather_fusion.4 = bf16[4096,128]{1,0:T(8,128)(2,1)} fusion(bf16[4096,128]{1,0:T(8,128)(2,1)S(1)} %bitcast.25, s32[4096]{0:T(1024)S(1)} %fusion.7), kind=kCustom, calls=%fused_computation.4 | custom fusion | bytes 2113536 | tf_op jit(solution)/shard_map/gather | solution.py:86
  (94 shorter events, 10.1 us)
Async XLA Ops:
  0.6 83.7 %copy-start = (bf16[4096,128]{1,0:T(8,128)(2,1)S(1)}, bf16[4096,128]{1,0:T(8,128)(2,1)}, u32[]{:S(2)}) copy-start(bf16[4096,128]{1,0:T(8,128)(2,1)} %param.8) | copy-start | bytes 3145732
  0.6 6.6 %copy-start.1 = (s32[4096]{0:T(1024)S(1)}, s32[4096]{0:T(1024)}, u32[]{:S(2)}) copy-start(s32[4096]{0:T(1024)} %param.11) | copy-start | bytes 49156
  7.3 23.1 %copy-start.2 = (s32[4096]{0:T(1024)S(1)}, s32[4096]{0:T(1024)}, u32[]{:S(2)}) copy-start(s32[4096]{0:T(1024)} %param.10) | copy-start | bytes 49156
  30.3 23.1 %copy-start.3 = (s32[4096]{0:T(1024)S(1)}, s32[4096]{0:T(1024)}, u32[]{:S(2)}) copy-start(s32[4096]{0:T(1024)} %param.9) | copy-start | bytes 49156
  77.1 22.3 %all-to-all-start = ((s32[8,4,3,128]{3,1,2,0:T(4,128)}), s32[8,4,3,128]{3,1,2,0:T(4,128)S(1)}, u32[]{:S(2)}, u32[]{:S(2)}) async-start(s32[8,4,3,128]{3,1,2,0:T(4,128)} %pad_add_fusion), calls=%async_computation | async-start | bytes 98304 | tf_op jit(solution)/shard_map/all_to_all | solution.py:43
  99.4 31.4 %all-to-all-start.2 = ((bf16[8,4,128,128]{3,2,1,0:T(8,128)(2,1)}), bf16[8,4,128,128]{3,2,1,0:T(8,128)(2,1)S(1)}, u32[]{:S(2)}, u32[]{:S(2)}) async-start(bf16[8,4,128,128]{3,2,1,0:T(8,128)(2,1)} %bitcast.6), calls=%async_computation.2 | async-start | bytes 2097152 | tf_op jit(solution)/shard_map/all_to_all | solution.py:36
  130.8 7.3 %all-to-all-start.1 = ((s32[8,4,3,128]{3,0,2,1:T(8,128)}), s32[8,4,3,128]{3,0,2,1:T(8,128)S(1)}, u32[]{:S(2)}, u32[]{:S(2)}) async-start(s32[8,4,3,128]{3,0,2,1:T(8,128)} %copy.38), calls=%async_computation.1 | async-start | bytes 98304 | tf_op jit(solution)/shard_map/all_to_all | solution.py:42
  138.1 17.9 %all-to-all-start.3 = ((bf16[8,4,128,128]{3,2,0,1:T(8,128)(2,1)}), bf16[8,4,128,128]{3,2,0,1:T(8,128)(2,1)S(1)}, u32[]{:S(2)}, u32[]{:S(2)}) async-start(bf16[8,4,128,128]{3,2,0,1:T(8,128)(2,1)} %copy.42), calls=%async_computation.3 | async-start | bytes 2097152 | tf_op jit(solution)/shard_map/all_to_all | solution.py:35
  163.9 1.2 copy-start.4
  172.9 1.2 copy-start.4
  181.8 1.2 copy-start.4
  190.7 1.2 copy-start.4
  199.6 1.2 copy-start.4
  208.5 1.2 copy-start.4
  217.4 1.2 copy-start.4
  226.3 1.2 copy-start.4
  259.6 50.9 %all-to-all-start.5 = ((bf16[8,4,128,128]{3,2,0,1:T(8,128)(2,1)}), bf16[8,4,128,128]{3,2,0,1:T(8,128)(2,1)S(1)}, u32[]{:S(2)}, u32[]{:S(2)}) async-start(bf16[8,4,128,128]{3,2,0,1:T(8,128)(2,1)} %copy.47), calls=%async_computation.5 | async-start | bytes 2097152 | tf_op jit(solution)/shard_map/all_to_all | solution.py:79
where the time goes:
time: 328 us; the launch traced here: 327 us
  local copies, waits for them, and re-layouts  107 us (33%)
  blocking collectives  70.1 us (21%)
  other arithmetic  60 us (18%)
  waiting for transfers between devices  42.1 us (13%)
  starting transfers between devices  23.6 us (7%)
  matrix products  15.4 us (5%)
  loops' own time  5.75 us (2%)
    psum x1, blocking collectives, on_device(): overall = lax.psum(duplicate_total, ('wide', 'narrow'))  40.9 us
    reduce_or x8, other arithmetic, full_block(): jnp.any(earlier, axis=1).astype(jnp.float32)  33 us
    all_to_all x1, blocking collectives, on_device(): lax.all_to_all(back_rows, 'wide', split_axis=0, concat_axis=0, tiled=True)  29.2 us
    all_to_all x1, waiting for transfers between devices, on_device(): lax.all_to_all(sent_rows, 'wide', split_axis=0, concat_axis=0, tiled=True)  24.8 us
    gather x1, local copies, waits for them, and re-layouts, on_device(): live[sort_order].reshape(shaped)  23 us
    gather x1, local copies, waits for them, and re-layouts, on_device(): second_key[sort_order].reshape(shaped)  23 us
    gather x1, local copies, waits for them, and re-layouts, on_device(): first_key[sort_order].reshape(shaped)  23 us
    dot_general x8, matrix products, full_block(): jnp.dot(same.astype(jnp.bfloat16), flat_rows, preferred_element_type=jnp....  15.4 us
  transfers between devices with their start and end apart: 5, of which 3 were waited for; matrix products, arithmetic and copies ran while one was open for 7% of the time, Pallas kernels for 0%

commit v1 on v0

--- a/solution.py
+++ b/solution.py
@@ -2,6 +2,30 @@
 import jax.numpy as jnp
 from jax import lax
 from jax.sharding import PartitionSpec as P
+
+
+def cut_along(x, dim, size):
+    shape = x.shape
+    pieces = x.reshape(*shape[:dim], size, shape[dim] // size, *shape[dim + 1 :])
+    return jnp.moveaxis(pieces, dim, 0)
+
+
+def joined_along(pieces, dim):
+    pieces = jnp.moveaxis(pieces, 0, dim)
+    shape = pieces.shape
+    return pieces.reshape(*shape[:dim], shape[dim] * shape[dim + 1], *shape[dim + 2 :])
+
+
+def rotated_exchange(array, axis, split_dim, concat_dim):
+    size, index = (lax.axis_size(axis), lax.axis_index(axis))
+    blocks = cut_along(array, split_dim, size)
+    out = blocks
+    for step in range(1, size):
+        target, source = ((index + step) % size, (index - step) % size)
+        sent = lax.dynamic_index_in_dim(blocks, target, 0)
+        partner_block = lax.ppermute(sent, axis, [(i, (i + step) % size) for i in range(size)])
+        out = lax.dynamic_update_slice_in_dim(out, partner_block, source, axis=0)
+    return joined_along(out, concat_dim)
 
 
 def pair_mask(row_one, row_two, row_live, col_one, col_two, col_live):
@@ -77,11 +101,7 @@
     )
     back_rows = group_means.reshape(wide_count, narrow_count, slot_rows, feature_cols)
     returned = lax.all_to_all(
-        lax.all_to_all(back_rows, "wide", split_axis=0, concat_axis=0, tiled=True),
-        "narrow",
-        split_axis=1,
-        concat_axis=1,
-        tiled=True,
+        rotated_exchange(back_rows, "wide", 0, 0), "narrow", split_axis=1, concat_axis=1, tiled=True
     )
     group_mean = returned.reshape(row_count, feature_cols)[inverse]
     overall = lax.psum(duplicate_total, ("wide", "narrow"))

time: 328 us -> 316 us (0.963)
  blocking collectives: 70.1 us -> 48.5 us
  waiting for transfers between devices: 42.1 us -> 51.9 us
  starting transfers between devices: 23.6 us -> 32.7 us
  matrix products: 15.4 us -> 10.6 us
    all_to_all x1 -> x0, blocking collectives: 29.2 us -> none  [on_device(): lax.all_to_all(back_rows, 'wide', split_axis=0, concat_axis=0, tiled=True)]
    ppermute x0 -> x7, waiting for transfers between devices: none -> 9.96 us  [rotated_exchange(): lax.ppermute(sent, axis, [(i, (i + step) % size) for i in range(size)])]
    ppermute x0 -> x7, starting transfers between devices: none -> 9.12 us  [rotated_exchange(): lax.ppermute(sent, axis, [(i, (i + step) % size) for i in range(size)])]
    psum x1, blocking collectives: 40.9 us -> 48.5 us  [on_device(): overall = lax.psum(duplicate_total, ('wide', 'narrow'))]
    dot_general x8, matrix products: 15.4 us -> 10.6 us  [full_block(): jnp.dot(same.astype(jnp.bfloat16), flat_rows, preferred_element_type=jnp....]
  transfers between devices with their start and end apart: 5 -> 12, of which waited for: 3 -> 6; matrix products, arithmetic and copies ran while one was open for 7% -> 7% of each run, Pallas kernels for 0% -> 0%
where the time goes in v1:
time: 316 us; the launch traced here: 315 us
  local copies, waits for them, and re-layouts  104 us (33%)
  other arithmetic  59.5 us (19%)
  waiting for transfers between devices  51.9 us (16%)
  blocking collectives  48.5 us (15%)
  starting transfers between devices  32.7 us (10%)
  matrix products  10.6 us (3%)
  loops' own time  5.6 us (2%)
    psum x1, blocking collectives, on_device(): overall = lax.psum(duplicate_total, ('wide', 'narrow'))  48.5 us
    reduce_or x8, other arithmetic, full_block(): jnp.any(earlier, axis=1).astype(jnp.float32)  32.9 us
    all_to_all x1, waiting for transfers between devices, on_device(): lax.all_to_all(sent_rows, 'wide', split_axis=0, concat_axis=0, tiled=True)  24.8 us
    gather x1, local copies, waits for them, and re-layouts, on_device(): live[sort_order].reshape(shaped)  23 us
    gather x1, local copies, waits for them, and re-layouts, on_device(): second_key[sort_order].reshape(shaped)  23 us
    gather x1, local copies, waits for them, and re-layouts, on_device(): first_key[sort_order].reshape(shaped)  23 us
    gather x1, local copies, waits for them, and re-layouts, on_device(): payload[sort_order]  15 us
    gather x1, local copies, waits for them, and re-layouts, on_device(): group_mean = returned.reshape(row_count, feature_cols)[inverse]  15 us
  transfers between devices with their start and end apart: 12, of which 6 were waited for; matrix products, arithmetic and copies ran while one was open for 7% of the time, Pallas kernels for 0%

profile of v1, /device:TPU:0, one launch (start us, length us, event | category | flops | bytes accessed | tf_op | source)
XLA Modules:
  0.0 315.4 jit_solution(13931927079038408655)
XLA Ops:
  1.5 5.8 %sort.31 = (s32[4096]{0:T(1024)}, s32[4096]{0:T(1024)S(1)}) sort(s32[4096]{0:T(1024)S(1)} %multiply_add_fusion, s32[4096]{0:T(1024)S(1)} %iota.19), dimensions={0}, to_apply=%region_0.0 | sort | flops 49152 | bytes 65536 | tf_op jit(solution)/shard_map/jit(argsort)/sort | solution.py:46
  7.3 23.0 %gather_fusion.2 = s32[4096]{0:T(1024)S(1)} fusion(s32[4096]{0:T(1024)S(1)} %copy-done.1, s32[4096]{0:T(1024)S(1)} %fusion.6), kind=kCustom, calls=%fused_computation.2 | custom fusion | bytes 49152 | tf_op jit(solution)/shard_map/gather | solution.py:54
  30.4 23.0 %gather_fusion.1 = s32[4096]{0:T(1024)S(1)} fusion(s32[4096]{0:T(1024)S(1)} %copy-done.2, s32[4096]{0:T(1024)S(1)} %fusion.6), kind=kCustom, calls=%fused_computation.1 | custom fusion | bytes 49152 | tf_op jit(solution)/shard_map/gather | solution.py:53
  53.4 23.0 %gather_fusion = s32[4096]{0:T(1024)S(1)} fusion(s32[4096]{0:T(1024)S(1)} %copy-done.3, s32[4096]{0:T(1024)S(1)} %fusion.6), kind=kCustom, calls=%fused_computation | custom fusion | bytes 49152 | tf_op jit(solution)/shard_map/gather | solution.py:52
  77.1 7.3 %all-to-all-start = ((s32[8,4,3,128]{3,1,2,0:T(4,128)}), s32[8,4,3,128]{3,1,2,0:T(4,128)S(1)}, u32[]{:S(2)}, u32[]{:S(2)}) async-start(s32[8,4,3,128]{3,1,2,0:T(4,128)} %pad_add_fusion), calls=%async_computation | async-start | bytes 98304 | tf_op jit(solution)/shard_map/all_to_all | solution.py:67
  84.4 15.0 %gather_fusion.3 = bf16[4096,128]{1,0:T(8,128)(2,1)} fusion(bf16[4096,128]{1,0:T(8,128)(2,1)S(1)} %copy-done, s32[4096]{0:T(1024)S(1)} %fusion.6), kind=kCustom, calls=%fused_computation.3 | custom fusion | bytes 2113536 | tf_op jit(solution)/shard_map/gather | solution.py:48
  99.4 6.0 %all-to-all-start.2 = ((bf16[8,4,128,128]{3,2,1,0:T(8,128)(2,1)}), bf16[8,4,128,128]{3,2,1,0:T(8,128)(2,1)S(1)}, u32[]{:S(2)}, u32[]{:S(2)}) async-start(bf16[8,4,128,128]{3,2,1,0:T(8,128)(2,1)} %bitcast.6), calls=%async_computation.2 | async-start | bytes 2097152 | tf_op jit(solution)/shard_map/all_to_all | solution.py:60
  106.0 24.8 %all-to-all-done.2 = bf16[8,4,128,128]{3,2,1,0:T(8,128)(2,1)S(1)} async-done(((bf16[8,4,128,128]{3,2,1,0:T(8,128)(2,1)}), bf16[8,4,128,128]{3,2,1,0:T(8,128)(2,1)S(1)}, u32[]{:S(2)}, u32[]{:S(2)}) %all-to-all-start.2) | async-done | bytes 1048608 | tf_op jit(solution)/shard_map/all_to_all | solution.py:60
  130.8 3.3 %all-to-all-start.1 = ((s32[8,4,3,128]{3,0,2,1:T(8,128)}), s32[8,4,3,128]{3,0,2,1:T(8,128)S(1)}, u32[]{:S(2)}, u32[]{:S(2)}) async-start(s32[8,4,3,128]{3,0,2,1:T(8,128)} %copy.58), calls=%async_computation.1 | async-start | bytes 98304 | tf_op jit(solution)/shard_map/all_to_all | solution.py:66
  134.1 1.0 copy.62
  135.1 3.0 all-to-all-done.1
  138.1 3.5 %all-to-all-start.3 = ((bf16[8,4,128,128]{3,2,0,1:T(8,128)(2,1)}), bf16[8,4,128,128]{3,2,0,1:T(8,128)(2,1)S(1)}, u32[]{:S(2)}, u32[]{:S(2)}) async-start(bf16[8,4,128,128]{3,2,0,1:T(8,128)(2,1)} %copy.62), calls=%async_computation.3 | async-start | bytes 2097152 | tf_op jit(solution)/shard_map/all_to_all | solution.py:59
  141.8 14.2 %all-to-all-done.3 = bf16[8,4,128,128]{3,2,0,1:T(8,128)(2,1)S(1)} async-done(((bf16[8,4,128,128]{3,2,0,1:T(8,128)(2,1)}), bf16[8,4,128,128]{3,2,0,1:T(8,128)(2,1)S(1)}, u32[]{:S(2)}, u32[]{:S(2)}) %all-to-all-start.3) | async-done | bytes 1048608 | tf_op jit(solution)/shard_map/all_to_all | solution.py:59
  156.3 63.9 %while.16 = (s32[]{:T(128)}, bf16[4096,128]{1,0:T(8,128)(2,1)S(1)}, f32[]{:T(128)}, s32[4096]{0:T(1024)S(1)}, s32[8,4,1,128]{3,2,1,0:T(1,128)S(1)}, /*index=5*/s...) while((s32[]{:T(128)}, bf16[4096,128]{1,0:T(8,128)(2,1)S(1)}, ...), condition=%wide.region_5.6_spmd.clone, body=%wide.region_1.5_spmd.clone.sunk | while | flops 557979136 | bytes 7557343 | solution.py:99
  156.6 4.1 %fusion.17 = (pred[512]{0:T(512)(128)(4,1)S(1)}, pred[512,4096]{1,0:T(32,128)(4,1)S(1)}) fusion(s32[512]{0:T(512)S(1)} %iota_add_fusion.2, pred[4096]{0:T(1024)(128)(4,1)S(1)} %bitcast.49, pred[512]{0:T(512)(128)(4,1)S(1)} %dynamic-slice_compare_fusion.2, s32[4096]{0:T(1024)S(1)} %bitcast.48, s32[512]{0:T(512)S(1)} %dynamic_slice.65, ...), kind=kLoop, calls=%fused_computation.9.clone.1 | loop fusion | flops 16776704 | bytes 2141184 | tf_op jit(solution)/shard_map/while/body/eval_jaxpr/reduce_or | solution.py:93
  160.7 1.0 convert_reduce_fusion.4
  161.7 1.3 fusion.18
  164.5 4.1 %fusion.17 = (pred[512]{0:T(512)(128)(4,1)S(1)}, pred[512,4096]{1,0:T(32,128)(4,1)S(1)}) fusion(s32[512]{0:T(512)S(1)} %iota_add_fusion.2, pred[4096]{0:T(1024)(128)(4,1)S(1)} %bitcast.49, pred[512]{0:T(512)(128)(4,1)S(1)} %dynamic-slice_compare_fusion.2, s32[4096]{0:T(1024)S(1)} %bitcast.48, s32[512]{0:T(512)S(1)} %dynamic_slice.65, ...), kind=kLoop, calls=%fused_computation.9.clone.1 | loop fusion | flops 16776704 | bytes 2141184 | tf_op jit(solution)/shard_map/while/body/eval_jaxpr/reduce_or | solution.py:93
  168.7 1.0 convert_reduce_fusion.4
  169.7 1.3 fusion.18
  172.5 4.1 %fusion.17 = (pred[512]{0:T(512)(128)(4,1)S(1)}, pred[512,4096]{1,0:T(32,128)(4,1)S(1)}) fusion(s32[512]{0:T(512)S(1)} %iota_add_fusion.2, pred[4096]{0:T(1024)(128)(4,1)S(1)} %bitcast.49, pred[512]{0:T(512)(128)(4,1)S(1)} %dynamic-slice_compare_fusion.2, s32[4096]{0:T(1024)S(1)} %bitcast.48, s32[512]{0:T(512)S(1)} %dynamic_slice.65, ...), kind=kLoop, calls=%fused_computation.9.clone.1 | loop fusion | flops 16776704 | bytes 2141184 | tf_op jit(solution)/shard_map/while/body/eval_jaxpr/reduce_or | solution.py:93
  176.6 1.0 convert_reduce_fusion.4
  177.6 1.3 fusion.18
  180.5 4.1 %fusion.17 = (pred[512]{0:T(512)(128)(4,1)S(1)}, pred[512,4096]{1,0:T(32,128)(4,1)S(1)}) fusion(s32[512]{0:T(512)S(1)} %iota_add_fusion.2, pred[4096]{0:T(1024)(128)(4,1)S(1)} %bitcast.49, pred[512]{0:T(512)(128)(4,1)S(1)} %dynamic-slice_compare_fusion.2, s32[4096]{0:T(1024)S(1)} %bitcast.48, s32[512]{0:T(512)S(1)} %dynamic_slice.65, ...), kind=kLoop, calls=%fused_computation.9.clone.1 | loop fusion | flops 16776704 | bytes 2141184 | tf_op jit(solution)/shard_map/while/body/eval_jaxpr/reduce_or | solution.py:93
  184.6 1.0 convert_reduce_fusion.4
  185.6 1.3 fusion.18
  188.5 4.1 %fusion.17 = (pred[512]{0:T(512)(128)(4,1)S(1)}, pred[512,4096]{1,0:T(32,128)(4,1)S(1)}) fusion(s32[512]{0:T(512)S(1)} %iota_add_fusion.2, pred[4096]{0:T(1024)(128)(4,1)S(1)} %bitcast.49, pred[512]{0:T(512)(128)(4,1)S(1)} %dynamic-slice_compare_fusion.2, s32[4096]{0:T(1024)S(1)} %bitcast.48, s32[512]{0:T(512)S(1)} %dynamic_slice.65, ...), kind=kLoop, calls=%fused_computation.9.clone.1 | loop fusion | flops 16776704 | bytes 2141184 | tf_op jit(solution)/shard_map/while/body/eval_jaxpr/reduce_or | solution.py:93
  193.6 1.3 fusion.18
  196.5 4.1 %fusion.17 = (pred[512]{0:T(512)(128)(4,1)S(1)}, pred[512,4096]{1,0:T(32,128)(4,1)S(1)}) fusion(s32[512]{0:T(512)S(1)} %iota_add_fusion.2, pred[4096]{0:T(1024)(128)(4,1)S(1)} %bitcast.49, pred[512]{0:T(512)(128)(4,1)S(1)} %dynamic-slice_compare_fusion.2, s32[4096]{0:T(1024)S(1)} %bitcast.48, s32[512]{0:T(512)S(1)} %dynamic_slice.65, ...), kind=kLoop, calls=%fused_computation.9.clone.1 | loop fusion | flops 16776704 | bytes 2141184 | tf_op jit(solution)/shard_map/while/body/eval_jaxpr/reduce_or | solution.py:93
  201.6 1.3 fusion.18
  204.5 4.1 %fusion.17 = (pred[512]{0:T(512)(128)(4,1)S(1)}, pred[512,4096]{1,0:T(32,128)(4,1)S(1)}) fusion(s32[512]{0:T(512)S(1)} %iota_add_fusion.2, pred[4096]{0:T(1024)(128)(4,1)S(1)} %bitcast.49, pred[512]{0:T(512)(128)(4,1)S(1)} %dynamic-slice_compare_fusion.2, s32[4096]{0:T(1024)S(1)} %bitcast.48, s32[512]{0:T(512)S(1)} %dynamic_slice.65, ...), kind=kLoop, calls=%fused_computation.9.clone.1 | loop fusion | flops 16776704 | bytes 2141184 | tf_op jit(solution)/shard_map/while/body/eval_jaxpr/reduce_or | solution.py:93
  208.6 1.0 convert_reduce_fusion.4
  209.6 1.3 fusion.18
  212.4 4.1 %fusion.17 = (pred[512]{0:T(512)(128)(4,1)S(1)}, pred[512,4096]{1,0:T(32,128)(4,1)S(1)}) fusion(s32[512]{0:T(512)S(1)} %iota_add_fusion.2, pred[4096]{0:T(1024)(128)(4,1)S(1)} %bitcast.49, pred[512]{0:T(512)(128)(4,1)S(1)} %dynamic-slice_compare_fusion.2, s32[4096]{0:T(1024)S(1)} %bitcast.48, s32[512]{0:T(512)S(1)} %dynamic_slice.65, ...), kind=kLoop, calls=%fused_computation.9.clone.1 | loop fusion | flops 16776704 | bytes 2141184 | tf_op jit(solution)/shard_map/while/body/eval_jaxpr/reduce_or | solution.py:93
  216.6 1.0 convert_reduce_fusion.4
  217.6 1.3 fusion.18
  220.3 1.3 collective-permute-start
  221.5 1.7 collective-permute-start.2
  223.3 2.3 collective-permute-start.3
  225.6 1.8 collective-permute-start.4
  227.4 2.2 collective-permute-done
  229.8 2.0 collective-permute-start.6
  231.8 7.5 %collective-permute-done.2 = bf16[1,1,4,128,128]{4,3,2,1,0:T(8,128)(2,1)S(1)} collective-permute-done((bf16[1,1,4,128,128]{4,3,2,1,0:T(8,128)(2,1)S(1)}, bf16[1,1,4,128,128]{4,3,2,1,0:T(8,128)(2,1)S(1)}, u32[]{:S(2)}, u32[]{:S(2)}) %collective-permute-start.2) | collective-permute-done | bytes 131104 | tf_op jit(solution)/shard_map/ppermute | solution.py:26
  239.6 1.0 copy.67
  240.6 3.5 %all-to-all-start.4 = ((bf16[8,4,128,128]{3,2,0,1:T(8,128)(2,1)}), bf16[8,4,128,128]{3,2,0,1:T(8,128)(2,1)S(1)}, u32[]{:S(2)}, u32[]{:S(2)}) async-start(bf16[8,4,128,128]{3,2,0,1:T(8,128)(2,1)} %copy.67), calls=%async_computation.4 | async-start | bytes 2097152 | tf_op jit(solution)/shard_map/all_to_all | solution.py:103
  244.1 5.8 %sort.32 = (s32[4096]{0:T(1024)}, s32[4096]{0:T(1024)S(1)}) sort(s32[4096]{0:T(1024)S(1)} %get-tuple-element.189, s32[4096]{0:T(1024)S(1)} %iota.21), dimensions={0}, to_apply=%region_6.7 | sort | flops 49152 | bytes 65536 | tf_op jit(solution)/shard_map/jit(argsort)/sort | solution.py:47
  249.9 48.5 %psum.7 = f32[]{:T(128)} all-reduce(f32[]{:T(128)} %get-tuple-element.192), channel_id=1, replica_groups=mesh['wide'=8,'narrow'=4] {'wide','narrow'}, use_global_device_ids=true, to_apply=%region_7.8 | all-reduce | flops 1 | bytes 8 | tf_op jit(solution)/shard_map/psum | solution.py:107
  299.2 15.0 %gather_fusion.4 = bf16[4096,128]{1,0:T(8,128)(2,1)} fusion(bf16[4096,128]{1,0:T(8,128)(2,1)S(1)} %bitcast.40, s32[4096]{0:T(1024)S(1)} %fusion.7), kind=kCustom, calls=%fused_computation.4 | custom fusion | bytes 2113536 | tf_op jit(solution)/shard_map/gather | solution.py:106
  (99 shorter events, 11.9 us)
Async XLA Ops:
  0.6 83.7 %copy-start = (bf16[4096,128]{1,0:T(8,128)(2,1)S(1)}, bf16[4096,128]{1,0:T(8,128)(2,1)}, u32[]{:S(2)}) copy-start(bf16[4096,128]{1,0:T(8,128)(2,1)} %param.8) | copy-start | bytes 3145732
  0.6 6.6 %copy-start.1 = (s32[4096]{0:T(1024)S(1)}, s32[4096]{0:T(1024)}, u32[]{:S(2)}) copy-start(s32[4096]{0:T(1024)} %param.11) | copy-start | bytes 49156
  7.3 23.1 %copy-start.2 = (s32[4096]{0:T(1024)S(1)}, s32[4096]{0:T(1024)}, u32[]{:S(2)}) copy-start(s32[4096]{0:T(1024)} %param.10) | copy-start | bytes 49156
  30.3 23.1 %copy-start.3 = (s32[4096]{0:T(1024)S(1)}, s32[4096]{0:T(1024)}, u32[]{:S(2)}) copy-start(s32[4096]{0:T(1024)} %param.9) | copy-start | bytes 49156
  77.1 22.3 %all-to-all-start = ((s32[8,4,3,128]{3,1,2,0:T(4,128)}), s32[8,4,3,128]{3,1,2,0:T(4,128)S(1)}, u32[]{:S(2)}, u32[]{:S(2)}) async-start(s32[8,4,3,128]{3,1,2,0:T(4,128)} %pad_add_fusion), calls=%async_computation | async-start | bytes 98304 | tf_op jit(solution)/shard_map/all_to_all | solution.py:67
  99.4 31.4 %all-to-all-start.2 = ((bf16[8,4,128,128]{3,2,1,0:T(8,128)(2,1)}), bf16[8,4,128,128]{3,2,1,0:T(8,128)(2,1)S(1)}, u32[]{:S(2)}, u32[]{:S(2)}) async-start(bf16[8,4,128,128]{3,2,1,0:T(8,128)(2,1)} %bitcast.6), calls=%async_computation.2 | async-start | bytes 2097152 | tf_op jit(solution)/shard_map/all_to_all | solution.py:60
  130.8 7.3 %all-to-all-start.1 = ((s32[8,4,3,128]{3,0,2,1:T(8,128)}), s32[8,4,3,128]{3,0,2,1:T(8,128)S(1)}, u32[]{:S(2)}, u32[]{:S(2)}) async-start(s32[8,4,3,128]{3,0,2,1:T(8,128)} %copy.58), calls=%async_computation.1 | async-start | bytes 98304 | tf_op jit(solution)/shard_map/all_to_all | solution.py:66
  138.1 17.9 %all-to-all-start.3 = ((bf16[8,4,128,128]{3,2,0,1:T(8,128)(2,1)}), bf16[8,4,128,128]{3,2,0,1:T(8,128)(2,1)S(1)}, u32[]{:S(2)}, u32[]{:S(2)}) async-start(bf16[8,4,128,128]{3,2,0,1:T(8,128)(2,1)} %copy.62), calls=%async_computation.3 | async-start | bytes 2097152 | tf_op jit(solution)/shard_map/all_to_all | solution.py:59
  220.3 9.3 %collective-permute-start = (bf16[1,1,4,128,128]{4,3,2,1,0:T(8,128)(2,1)S(1)}, bf16[1,1,4,128,128]{4,3,2,1,0:T(8,128)(2,1)S(1)}, u32[]{:S(2)}, u32[]{:S(2)}) collective-permute-start(bf16[1,1,4,128,128]{4,3,2,1,0:T(8,128)(2,1)S(1)} %get-tuple-element.293), channel_id=1, source_target_pairs={{0,4},{4,8},{8,12},{12,16},{16,20},{20,24},{24,28},{28,0},{1,5},{5... | collective-permute-start | bytes 393224 | tf_op jit(solution)/shard_map/ppermute | solution.py:26
  221.5 8.3 %collective-permute-start.1 = (bf16[1,1,4,128,128]{4,3,2,1,0:T(8,128)(2,1)S(1)}, bf16[1,1,4,128,128]{4,3,2,1,0:T(8,128)(2,1)S(1)}, u32[]{:S(2)}, u32[]{:S(2)}) collective-permute-start(bf16[1,1,4,128,128]{4,3,2,1,0:T(8,128)(2,1)S(1)} %get-tuple-element.292), channel_id=1, source_target_pairs={{0,8},{4,12},{8,16},{12,20},{16,24},{20,28},{24,0},{28,4},{1,9},{5... | collective-permute-start | bytes 393224 | tf_op jit(solution)/shard_map/ppermute | solution.py:26
  221.5 17.8 %collective-permute-start.2 = (bf16[1,1,4,128,128]{4,3,2,1,0:T(8,128)(2,1)S(1)}, bf16[1,1,4,128,128]{4,3,2,1,0:T(8,128)(2,1)S(1)}, u32[]{:S(2)}, u32[]{:S(2)}) collective-permute-start(bf16[1,1,4,128,128]{4,3,2,1,0:T(8,128)(2,1)S(1)} %get-tuple-element.291), channel_id=1, source_target_pairs={{0,12},{4,16},{8,20},{12,24},{16,28},{20,0},{24,4},{28,8},{1,13},{... | collective-permute-start | bytes 393224 | tf_op jit(solution)/shard_map/ppermute | solution.py:26
  223.3 16.1 %collective-permute-start.3 = (bf16[1,1,4,128,128]{4,3,2,1,0:T(8,128)(2,1)S(1)}, bf16[1,1,4,128,128]{4,3,2,1,0:T(8,128)(2,1)S(1)}, u32[]{:S(2)}, u32[]{:S(2)}) collective-permute-start(bf16[1,1,4,128,128]{4,3,2,1,0:T(8,128)(2,1)S(1)} %get-tuple-element.290), channel_id=1, source_target_pairs={{0,16},{4,20},{8,24},{12,28},{16,0},{20,4},{24,8},{28,12},{1,17},{... | collective-permute-start | bytes 393224 | tf_op jit(solution)/shard_map/ppermute | solution.py:26
  225.6 13.8 %collective-permute-start.4 = (bf16[1,1,4,128,128]{4,3,2,1,0:T(8,128)(2,1)S(1)}, bf16[1,1,4,128,128]{4,3,2,1,0:T(8,128)(2,1)S(1)}, u32[]{:S(2)}, u32[]{:S(2)}) collective-permute-start(bf16[1,1,4,128,128]{4,3,2,1,0:T(8,128)(2,1)S(1)} %get-tuple-element.289), channel_id=1, source_target_pairs={{0,20},{4,24},{8,28},{12,0},{16,4},{20,8},{24,12},{28,16},{1,21},{... | collective-permute-start | bytes 393224 | tf_op jit(solution)/shard_map/ppermute | solution.py:26
  229.6 9.9 %collective-permute-start.5 = (bf16[1,1,4,128,128]{4,3,2,1,0:T(8,128)(2,1)S(1)}, bf16[1,1,4,128,128]{4,3,2,1,0:T(8,128)(2,1)S(1)}, u32[]{:S(2)}, u32[]{:S(2)}) collective-permute-start(bf16[1,1,4,128,128]{4,3,2,1,0:T(8,128)(2,1)S(1)} %get-tuple-element.288), channel_id=1, source_target_pairs={{0,24},{4,28},{8,0},{12,4},{16,8},{20,12},{24,16},{28,20},{1,25},{... | collective-permute-start | bytes 393224 | tf_op jit(solution)/shard_map/ppermute | solution.py:26
  229.8 9.7 %collective-permute-start.6 = (bf16[1,1,4,128,128]{4,3,2,1,0:T(8,128)(2,1)S(1)}, bf16[1,1,4,128,128]{4,3,2,1,0:T(8,128)(2,1)S(1)}, u32[]{:S(2)}, u32[]{:S(2)}) collective-permute-start(bf16[1,1,4,128,128]{4,3,2,1,0:T(8,128)(2,1)S(1)} %get-tuple-element.287), channel_id=1, source_target_pairs={{0,28},{4,0},{8,4},{12,8},{16,12},{20,16},{24,20},{28,24},{1,29},{... | collective-permute-start | bytes 393224 | tf_op jit(solution)/shard_map/ppermute | solution.py:26
  240.6 58.5 %all-to-all-start.4 = ((bf16[8,4,128,128]{3,2,0,1:T(8,128)(2,1)}), bf16[8,4,128,128]{3,2,0,1:T(8,128)(2,1)S(1)}, u32[]{:S(2)}, u32[]{:S(2)}) async-start(bf16[8,4,128,128]{3,2,0,1:T(8,128)(2,1)} %copy.67), calls=%async_computation.4 | async-start | bytes 2097152 | tf_op jit(solution)/shard_map/all_to_all | solution.py:103
